TPU v7x, 8 devices: a whole 2x2x1 slice. The times are simulated.
8 devices in a mesh: dp: 1 (over z), tp: 8 (over x, y, core).
Axes of the slice: x: 2, y: 2, z: 1, core: 2. Of those that a mesh axis runs over, the one named last changes fastest.
Arguments:
- x: bfloat16 [2048, 5376], P('dp')
- w_gate: bfloat16 [5376, 21504], P(None, 'tp')
- w_up: bfloat16 [5376, 21504], P(None, 'tp')
- w_down: bfloat16 [21504, 5376], P('tp')
Outputs:
- output: bfloat16 [2048, 5376], P('dp')
All inputs are finite; a program needn't handle non-finite values.
Results may differ from a plain program's by a relative error of at most 0.016.
Values are sent between devices in bfloat16 or wider.
A program may use at most 2 GiB of HBM per device.

v0:
```python
import jax
import jax.numpy as jnp
from jax import lax
from jax.sharding import PartitionSpec as P


def solution(mesh):
    def step(x, w_gate, w_up, w_down):
        gate = jnp.dot(x, w_gate, preferred_element_type=jnp.float32)
        up = jnp.dot(x, w_up, preferred_element_type=jnp.float32)
        hidden = (jax.nn.gelu(gate) * up).astype(jnp.bfloat16)
        term = jnp.dot(hidden, w_down, preferred_element_type=jnp.float32).astype(jnp.bfloat16)
        return lax.psum(term, "tp")

    return jax.shard_map(
        step,
        mesh=mesh,
        in_specs=(P("dp", None), P(None, "tp"), P(None, "tp"), P("tp", None)),
        out_specs=P("dp", None),
        check_vma=False,
    )
```

profile of v0, /device:TPU:0, one launch (start us, length us, event | category | flops | bytes accessed | tf_op | source)
XLA Modules:
  0.0 524.7 jit_solution(15903779764218502385)
XLA Ops:
  6.5 0.0 all-reduce.2.cloned.1.call-start
  6.5 76.3 %fusion.9 = f32[2048,2688]{1,0:T(8,128)} fusion(bf16[2048,5376]{1,0:T(8,128)(2,1)} %param.4, bf16[5376,2688]{1,0:T(8,128)(2,1)} %param.5), kind=kOutput, calls=%fused_computation.11 | convolution fusion | flops 59190018048 | bytes 72941568 | tf_op jit(solution)/shard_map/dot_general | solution.py:9
  82.9 81.0 %fusion.8 = bf16[2048,2688]{1,0:T(8,128)(2,1)} fusion(f32[2048,2688]{1,0:T(8,128)} %fusion.9, bf16[2048,5376]{1,0:T(8,128)(2,1)} %param.4, bf16[5376,2688]{1,0:T(8,128)(2,1)} %param.6), kind=kOutput, calls=%fused_computation.10 | convolution fusion | flops 59245068288 | bytes 83951616 | tf_op jit(solution)/shard_map/dot_general | solution.py:10
  163.9 70.7 %convolution_convert_fusion = bf16[2048,5376]{1,0:T(8,128)(2,1)} fusion(bf16[2048,2688]{1,0:T(8,128)(2,1)} %fusion.8, bf16[2688,5376]{1,0:T(8,128)(2,1)} %param.7), kind=kOutput, calls=%fused_computation.1 | convolution fusion | flops 59201028096 | bytes 61931520 | tf_op jit(solution)/shard_map/dot_general | solution.py:12
  234.6 0.0 all-reduce.2.cloned.1.call-update
  234.6 264.6 %all-reduce.2.cloned.1.call-done = bf16[2048,5376]{1,0:T(8,128)(2,1)} async-done(((bf16[2048,5376]{1,0:T(8,128)(2,1)}), bf16[2048,5376]{1,0:T(8,128)(2,1)}) %all-reduce.2.cloned.1.call-update) | async-done | bytes 22020112 | tf_op jit(solution)/shard_map/psum | solution.py:13
  499.2 18.6 %copy.6 = bf16[2048,5376]{1,0:T(8,128)(2,1)} copy(bf16[2048,5376]{1,0:T(8,128)(2,1)} %all-reduce.2.cloned.1.call-done) | data formatting | bytes 44040192
Async XLA Ops:
  6.5 492.6 %all-reduce.2.cloned.1.call-start = ((), (), s32[]{:S(2)}) async-start(), calls=%async_computation | async-start | bytes 44040192 | tf_op jit(solution)/shard_map/psum | solution.py:13
Sparse Core Ops, SparseCore 0:
  234.7 264.4 all-reduce.1
where the time goes:
time: 525 us
  waiting for transfers between devices  265 us (50%)
  matrix products  228 us (43%)
  local copies, waits for them, and re-layouts  18.6 us (4%)
  between operations  13.4 us (3%)
    psum x1, waiting for transfers between devices, step(): return lax.psum(term, 'tp')  265 us
    dot_general x1, matrix products, step(): up = jnp.dot(x, w_up, preferred_element_type=jnp.float32)  81 us
    dot_general x1, matrix products, step(): gate = jnp.dot(x, w_gate, preferred_element_type=jnp.float32)  76.3 us
    dot_general x1, matrix products, step(): jnp.dot(hidden, w_down, preferred_element_type=jnp.float32)  70.7 us
    unnamed x1, local copies, waits for them, and re-layouts  18.6 us
  transfers between devices with their start and end apart: 1, of which 1 were waited for; matrix products, arithmetic and copies ran while one was open for 0% of the time, Pallas kernels for 0%

commit v1 on v0

v1 whole, which is shorter than its diff:
```python
import jax
import jax.numpy as jnp
from jax import lax
from jax.experimental import pallas as pl
from jax.experimental.pallas import tpu as pltpu
from jax.sharding import PartitionSpec as P

MESH = pl.DeviceIdType.MESH
ROWS, D, FF = 2048, 5376, 2688
GROUP = 512
HALF, QUARTER, SIXTH = GROUP // 2, GROUP // 8, GROUP // 16
GROUPS = ROWS // GROUP
T1 = 384
T2 = 768
TILES = FF // T1
PERIOD = 2 * TILES
OFFSETS = (2, 4, 6, 8, 10, 12)
S0, S1, S2, G1, G2, G3 = 0, 1, 3, 5, 7, 9


def kernel(x_hbm, wg, wu, wd, y, xbuf, wbuf, wdbuf, hid, acc, s0s, s0r, s1s, s1r, s2s, s2r, fin, xsem, wsem, wdsem, ssem, rsem, lsem):
    me = lax.axis_index("tp")
    cx, cy, core = me // 4, (me // 2) % 2, me % 2
    pn = me + 1 - 2 * core
    xn = me + 4 - 8 * cx
    yn = me + 2 - 4 * cy

    barrier = pltpu.get_barrier_semaphore()
    for n in (pn, xn, yn):
        pl.semaphore_signal(barrier, inc=1, device_id={"tp": n}, device_id_type=MESH)
    pl.semaphore_wait(barrier, 3)

    a = lambda i, j: i * QUARTER + j * SIXTH
    b = lambda j, i: HALF // 2 + j * QUARTER + i * SIXTH
    blocks = (a(cx, cy), a(cx, 1 - cy), a(1 - cx, cy), a(1 - cx, 1 - cy), b(cy, cx), b(cy, 1 - cx), b(1 - cy, cx), b(1 - cy, 1 - cx))

    def x_copies(g):
        out = []
        for h, c in enumerate((core, 1 - core)):
            for k, off in enumerate(blocks):
                row = pl.multiple_of(g * GROUP + c * HALF + off, SIXTH)
                i = h * len(blocks) + k
                out.append(pltpu.make_async_copy(x_hbm.at[pl.ds(row, SIXTH)], xbuf.at[pl.ds(i * SIXTH, SIXTH)], xsem.at[i]))
        return out

    def w_copies(j, slot):
        cols = pl.ds(pl.multiple_of(j * T1, T1), T1)
        return [
            pltpu.make_async_copy(wg.at[:, cols], wbuf.at[slot, :, pl.ds(0, T1)], wsem.at[slot, 0]),
            pltpu.make_async_copy(wu.at[:, cols], wbuf.at[slot, :, pl.ds(T1, T1)], wsem.at[slot, 1]),
        ]

    def columns(j):
        return pl.ds(pl.multiple_of(j * T2, T2), T2)

    def wd_copy(j, slot):
        return pltpu.make_async_copy(wd.at[:, columns(j)], wdbuf.at[slot], wdsem.at[slot])

    def remote(src, dst, sem, j, to):
        return pltpu.make_async_remote_copy(src_ref=src, dst_ref=dst, send_sem=ssem.at[sem, j], recv_sem=rsem.at[sem, j], device_id={"tp": to}, device_id_type=MESH)

    def part(g, off, rows, j):
        return y.at[pl.ds(pl.multiple_of(g * GROUP + core * HALF + off, SIXTH), rows), columns(j)]

    def copies(stage, g, j):
        if stage == S0:
            return [remote(s0s.at[j], s0r.at[j], S0, j, pn)]
        if stage == S1:
            return [remote(s1s.at[j, i], s1r.at[j, i], S1 + i, j, (xn, yn)[i]) for i in range(2)]
        if stage == S2:
            return [remote(s2s.at[j, i], s2r.at[j, i], S2 + i, j, (yn, xn)[i]) for i in range(2)]
        if stage == G1:
            return [remote(fin.at[j, i], part(g, blocks[4 * i], SIXTH, j), G1 + i, j, (yn, xn)[i]) for i in range(2)]
        if stage == G2:
            offs = (cx * QUARTER, HALF // 2 + cy * QUARTER)
            return [remote(part(g, offs[i], QUARTER, j), part(g, offs[i], QUARTER, j), G2 + i, j, (xn, yn)[i]) for i in range(2)]
        return [remote(part(g, 0, HALF, j), part(g, 0, HALF, j), G3, j, pn)]

    def own(g, j):
        return [pltpu.make_async_copy(fin.at[j, i], part(g, blocks[4 * i], SIXTH, j), lsem.at[i, j]) for i in range(2)]

    def start(cs):
        for c in cs:
            c.start()

    def arrive(cs):
        for c in cs:
            c.wait_recv()

    f32, bf16 = jnp.float32, jnp.bfloat16
    Q, H = QUARTER, HALF // 2

    def stage1(g, j):
        arrive(copies(S0, g, j))
        for i in range(2):
            keep, send = pl.ds(i * H, Q), pl.ds(i * H + Q, Q)
            s1s[j, i] = (acc[j, send] + s0r[j, send].astype(f32)).astype(bf16)
            acc[j, keep] = acc[j, keep] + s0r[j, keep].astype(f32)
        start(copies(S1, g, j))

    def stage2(g, j):
        arrive(copies(S1, g, j))
        for i in range(2):
            keep, send = pl.ds(i * H, SIXTH), pl.ds(i * H + SIXTH, SIXTH)
            s2s[j, i] = (acc[j, send] + s1r[j, i, SIXTH:].astype(f32)).astype(bf16)
            acc[j, keep] = acc[j, keep] + s1r[j, i, :SIXTH].astype(f32)
        start(copies(S2, g, j))

    def stage3(g, j):
        arrive(copies(S2, g, j))
        for i in range(2):
            fin[j, i] = (acc[j, pl.ds(i * H, SIXTH)] + s2r[j, i].astype(f32)).astype(bf16)
        start(copies(G1, g, j))
        start(own(g, j))

    def stage4(g, j):
        for c in own(g, j):
            c.wait()
        arrive(copies(G1, g, j))
        start(copies(G2, g, j))

    def stage5(g, j):
        arrive(copies(G2, g, j))
        start(copies(G3, g, j))

    def stage6(g, j):
        arrive(copies(G3, g, j))
        for stage in (S0, S1, S2, G1, G2, G3):
            for c in copies(stage, g, j):
                c.wait_send()

    def service(tick):
        for fn, off in zip((stage1, stage2, stage3, stage4, stage5, stage6), OFFSETS):
            w = tick - TILES - off
            pos = lax.max(w, 0)
            g, j = pos // PERIOD, pos % PERIOD

            @pl.when((w >= 0) & (j < TILES) & (g < GROUPS))
            def _():
                fn(g, j)

    start(x_copies(0))
    start(w_copies(0, 0))
    wd_copy(0, 0).start()

    def group(g, _):
        for c in x_copies(g):
            c.wait()

        def first(j, _):
            n = g * TILES + j
            slot = n % 2

            @pl.when(n + 1 < GROUPS * TILES)
            def _():
                start(w_copies((j + 1) % TILES, 1 - slot))

            service(g * PERIOD + j)
            for c in w_copies(j, slot):
                c.wait()
            r = jnp.dot(xbuf[...], wbuf[slot], preferred_element_type=f32)
            hid[:, pl.ds(pl.multiple_of(j * T1, T1), T1)] = (jax.nn.gelu(r[:, :T1]) * r[:, T1:]).astype(bf16)
            return 0

        lax.fori_loop(0, TILES, first, 0)

        @pl.when(g + 1 < GROUPS)
        def _():
            start(x_copies(g + 1))

        def second(j, _):
            n = g * TILES + j
            slot = n % 2

            @pl.when(n + 1 < GROUPS * TILES)
            def _():
                wd_copy((j + 1) % TILES, 1 - slot).start()

            service(g * PERIOD + TILES + j)
            wd_copy(j, slot).wait()
            r = jnp.dot(hid[...], wdbuf[slot], preferred_element_type=f32)
            acc[j] = r[:HALF]
            s0s[j] = r[HALF:].astype(bf16)
            start(copies(S0, g, j))
            return 0

        lax.fori_loop(0, TILES, second, 0)
        return 0

    lax.fori_loop(0, GROUPS, group, 0)

    def drain(i, _):
        service(GROUPS * PERIOD + i)
        return 0

    lax.fori_loop(0, OFFSETS[-1], drain, 0)


def solution(mesh):
    bf16, f32 = jnp.bfloat16, jnp.float32

    def step(x, w_gate, w_up, w_down):
        return pl.pallas_call(
            kernel,
            out_shape=jax.ShapeDtypeStruct((ROWS, D), bf16),
            in_specs=[pl.BlockSpec(memory_space=pl.ANY)] * 4,
            out_specs=pl.BlockSpec(memory_space=pl.ANY),
            scratch_shapes=[
                pltpu.VMEM((GROUP, D), bf16),
                pltpu.VMEM((2, D, 2 * T1), bf16),
                pltpu.VMEM((2, FF, T2), bf16),
                pltpu.VMEM((GROUP, FF), bf16),
                pltpu.VMEM((TILES, HALF, T2), f32),
                pltpu.VMEM((TILES, HALF, T2), bf16),
                pltpu.VMEM((TILES, HALF, T2), bf16),
                pltpu.VMEM((TILES, 2, QUARTER, T2), bf16),
                pltpu.VMEM((TILES, 2, QUARTER, T2), bf16),
                pltpu.VMEM((TILES, 2, SIXTH, T2), bf16),
                pltpu.VMEM((TILES, 2, SIXTH, T2), bf16),
                pltpu.VMEM((TILES, 2, SIXTH, T2), bf16),
                pltpu.SemaphoreType.DMA((16,)),
                pltpu.SemaphoreType.DMA((2, 2)),
                pltpu.SemaphoreType.DMA((2,)),
                pltpu.SemaphoreType.DMA((10, TILES)),
                pltpu.SemaphoreType.DMA((10, TILES)),
                pltpu.SemaphoreType.DMA((2, TILES)),
            ],
            compiler_params=pltpu.CompilerParams(collective_id=0, has_side_effects=True, vmem_limit_bytes=67043328),
            cost_estimate=pl.CostEstimate(flops=6 * ROWS * D * FF, bytes_accessed=400 * 2**20, transcendentals=ROWS * FF),
        )(x, w_gate, w_up, w_down)

    return jax.shard_map(
        step,
        mesh=mesh,
        in_specs=(P("dp", None), P(None, "tp"), P(None, "tp"), P("tp", None)),
        out_specs=P("dp", None),
        check_vma=False,
    )
```

time: 525 us -> 273 us (0.52)
  waiting for transfers between devices: 265 us -> 0 us
  Pallas kernels: 0 us -> 254 us
  matrix products: 228 us -> 0 us
  between operations: 13.4 us -> 0.01 us
    psum x1 -> x0, waiting for transfers between devices: 265 us -> none  [step(): return lax.psum(term, 'tp')]
    pallas_call x0 -> x1, Pallas kernels: none -> 254 us  [step(): pl.pallas_call(kernel, out_shape=jax.ShapeDtypeStruct((ROWS, D), bf16), i...]
    dot_general x3 -> x0, matrix products: 228 us -> none  [the longest x1 81 us: step(): up = jnp.dot(x, w_up, preferred_element_type=jnp.float32)]
  transfers between devices with their start and end apart: 1 -> 0, of which waited for: 1 -> 0; matrix products, arithmetic and copies ran while one was open for 0% -> 0% of each run, Pallas kernels for 0% -> 0%
where the time goes in v1:
time: 273 us; the launch traced here: 272 us
  Pallas kernels  254 us (93%)
  local copies, waits for them, and re-layouts  18.7 us (7%)
    pallas_call x1, Pallas kernels, step(): pl.pallas_call(kernel, out_shape=jax.ShapeDtypeStruct((ROWS, D), bf16), i...  254 us
    unnamed x1, local copies, waits for them, and re-layouts  18.7 us

profile of v1, /device:TPU:0, one launch (start us, length us, event | category | flops | bytes accessed | tf_op | source)
XLA Modules:
  0.0 272.4 jit_solution(5959425700648796265)
XLA Ops:
  0.0 253.7 %shard_map.46 = bf16[2048,5376]{1,0:T(8,128)(2,1)} custom-call(bf16[2048,5376]{1,0:T(8,128)(2,1)} %x_hbm.1, bf16[5376,2688]{1,0:T(8,128)(2,1)} %wg.1, bf16[5376,2688]{1,0:T(8,128)(2,1)} %wu.1, bf16[2688,5376]{1,0:T(8,128)(2,1)} %wd.1), custom_call_target="tpu_custom_call" | custom-call | flops 177570054144 | bytes 419430400 | tf_op jit(solution)/shard_map/pallas_call | solution.py:203
  253.7 18.7 %copy.6 = bf16[2048,5376]{1,0:T(8,128)(2,1)} copy(bf16[2048,5376]{1,0:T(8,128)(2,1)} %shard_map.46) | data formatting | bytes 44040192

commit v2 on v1

--- a/solution.py
+++ b/solution.py
@@ -1,3 +1,5 @@
+import math
+
 import jax
 import jax.numpy as jnp
 from jax import lax
@@ -15,10 +17,25 @@
 TILES = FF // T1
 PERIOD = 2 * TILES
 OFFSETS = (2, 4, 6, 8, 10, 12)
+PIECES = 4
 S0, S1, S2, G1, G2, G3 = 0, 1, 3, 5, 7, 9
 
 
-def kernel(x_hbm, wg, wu, wd, y, xbuf, wbuf, wdbuf, hid, acc, s0s, s0r, s1s, s1r, s2s, s2r, fin, xsem, wsem, wdsem, ssem, rsem, lsem):
+def gelu(v):
+    c = (2 / math.pi) ** 0.5
+    return v * (0.5 + 0.5 * jnp.tanh(v * (c + (c * 0.044715) * (v * v))))
+
+
+def kernel(x_hbm, wg, wu, wd, y, whole, xbuf, wdbuf, hid, acc, s1s, s1r, s2s, s2r, fin, xsem, wsem, wdsem, ssem, rsem, lsem, vsem):
+    def wrows(slot):
+        return pl.ds(pl.multiple_of(slot * D, 128), D)
+
+    def srows(j, first=0, rows=HALF):
+        return pl.ds(pl.multiple_of(2 * D + j * HALF + first, QUARTER), rows)
+
+    def rrows(j, first=0, rows=HALF):
+        return pl.ds(pl.multiple_of(2 * D + TILES * HALF + j * HALF + first, QUARTER), rows)
+
     me = lax.axis_index("tp")
     cx, cy, core = me // 4, (me // 2) % 2, me % 2
     pn = me + 1 - 2 * core
@@ -46,8 +63,8 @@
     def w_copies(j, slot):
         cols = pl.ds(pl.multiple_of(j * T1, T1), T1)
         return [
-            pltpu.make_async_copy(wg.at[:, cols], wbuf.at[slot, :, pl.ds(0, T1)], wsem.at[slot, 0]),
-            pltpu.make_async_copy(wu.at[:, cols], wbuf.at[slot, :, pl.ds(T1, T1)], wsem.at[slot, 1]),
+            pltpu.make_async_copy(wg.at[:, cols], whole.at[wrows(slot), pl.ds(0, T1)], wsem.at[slot, 0]),
+            pltpu.make_async_copy(wu.at[:, cols], whole.at[wrows(slot), pl.ds(T1, T1)], wsem.at[slot, 1]),
         ]
 
     def columns(j):
@@ -64,7 +81,7 @@
 
     def copies(stage, g, j):
         if stage == S0:
-            return [remote(s0s.at[j], s0r.at[j], S0, j, pn)]
+            return [remote(whole.at[srows(j)], whole.at[rrows(j)], S0, j, pn)]
         if stage == S1:
             return [remote(s1s.at[j, i], s1r.at[j, i], S1 + i, j, (xn, yn)[i]) for i in range(2)]
         if stage == S2:
@@ -94,12 +111,14 @@
         arrive(copies(S0, g, j))
         for i in range(2):
             keep, send = pl.ds(i * H, Q), pl.ds(i * H + Q, Q)
-            s1s[j, i] = (acc[j, send] + s0r[j, send].astype(f32)).astype(bf16)
-            acc[j, keep] = acc[j, keep] + s0r[j, keep].astype(f32)
+            s1s[j, i] = (acc[j, send] + whole[rrows(j, i * H + Q, Q), :].astype(f32)).astype(bf16)
+            acc[j, keep] = acc[j, keep] + whole[rrows(j, i * H, Q), :].astype(f32)
         start(copies(S1, g, j))
 
     def stage2(g, j):
         arrive(copies(S1, g, j))
+        for c in copies(S0, g, j):
+            c.wait_send()
         for i in range(2):
             keep, send = pl.ds(i * H, SIXTH), pl.ds(i * H + SIXTH, SIXTH)
             s2s[j, i] = (acc[j, send] + s1r[j, i, SIXTH:].astype(f32)).astype(bf16)
@@ -125,7 +144,7 @@
 
     def stage6(g, j):
         arrive(copies(G3, g, j))
-        for stage in (S0, S1, S2, G1, G2, G3):
+        for stage in (S1, S2, G1, G2, G3):
             for c in copies(stage, g, j):
                 c.wait_send()
 
@@ -158,8 +177,8 @@
             service(g * PERIOD + j)
             for c in w_copies(j, slot):
                 c.wait()
-            r = jnp.dot(xbuf[...], wbuf[slot], preferred_element_type=f32)
-            hid[:, pl.ds(pl.multiple_of(j * T1, T1), T1)] = (jax.nn.gelu(r[:, :T1]) * r[:, T1:]).astype(bf16)
+            r = jnp.dot(xbuf[...], whole[wrows(slot), :], preferred_element_type=f32)
+            hid[:, pl.ds(pl.multiple_of(j * T1, T1), T1)] = (gelu(r[:, :T1]) * r[:, T1:]).astype(bf16)
             return 0
 
         lax.fori_loop(0, TILES, first, 0)
@@ -180,7 +199,7 @@
             wd_copy(j, slot).wait()
             r = jnp.dot(hid[...], wdbuf[slot], preferred_element_type=f32)
             acc[j] = r[:HALF]
-            s0s[j] = r[HALF:].astype(bf16)
+            whole[srows(j), :] = r[HALF:].astype(bf16)
             start(copies(S0, g, j))
             return 0
 
@@ -189,30 +208,54 @@
 
     lax.fori_loop(0, GROUPS, group, 0)
 
-    def drain(i, _):
+    def settle(j, first, rows, sem):
+        at = pl.ds(pl.multiple_of(j * ROWS + first, GROUP), rows)
+        return pltpu.make_async_copy(y.at[pl.ds(first, rows), columns(j)], whole.at[at], vsem.at[sem, j])
+
+    last, full = ROWS - GROUP, 2 * D // ROWS
+    for i in range(OFFSETS[-1]):
         service(GROUPS * PERIOD + i)
-        return 0
-
-    lax.fori_loop(0, OFFSETS[-1], drain, 0)
+        if i == 0:
+            for j in range(full):
+                settle(j, 0, last, 0).start()
+        if i == OFFSETS[1]:
+            for j in range(full, TILES):
+                settle(j, 0, last, 0).start()
+        j = i + TILES - OFFSETS[-1]
+        if j >= 0:
+            settle(j, last, GROUP, 1).start()
+    for j in range(TILES):
+        settle(j, 0, last, 0).wait()
+        settle(j, last, GROUP, 1).wait()
+
+
+def copy_kernel(whole, out, sem):
+    rows = ROWS // PIECES
+    cs = [
+        pltpu.make_async_copy(whole.at[pl.ds(j * ROWS + i * rows, rows)], out.at[pl.ds(i * rows, rows), pl.ds(j * T2, T2)], sem.at[j, i])
+        for i in range(PIECES)
+        for j in range(TILES)
+    ]
+    for c in cs:
+        c.start()
+    for c in cs:
+        c.wait()
 
 
 def solution(mesh):
     bf16, f32 = jnp.bfloat16, jnp.float32
 
     def step(x, w_gate, w_up, w_down):
-        return pl.pallas_call(
+        _, whole = pl.pallas_call(
             kernel,
-            out_shape=jax.ShapeDtypeStruct((ROWS, D), bf16),
+            out_shape=(jax.ShapeDtypeStruct((ROWS, D), bf16), pltpu.VMEM((TILES * ROWS, T2), bf16)),
             in_specs=[pl.BlockSpec(memory_space=pl.ANY)] * 4,
-            out_specs=pl.BlockSpec(memory_space=pl.ANY),
+            out_specs=(pl.BlockSpec(memory_space=pl.ANY), pl.BlockSpec(memory_space=pltpu.VMEM)),
             scratch_shapes=[
                 pltpu.VMEM((GROUP, D), bf16),
-                pltpu.VMEM((2, D, 2 * T1), bf16),
                 pltpu.VMEM((2, FF, T2), bf16),
                 pltpu.VMEM((GROUP, FF), bf16),
                 pltpu.VMEM((TILES, HALF, T2), f32),
-                pltpu.VMEM((TILES, HALF, T2), bf16),
-                pltpu.VMEM((TILES, HALF, T2), bf16),
                 pltpu.VMEM((TILES, 2, QUARTER, T2), bf16),
                 pltpu.VMEM((TILES, 2, QUARTER, T2), bf16),
                 pltpu.VMEM((TILES, 2, SIXTH, T2), bf16),
@@ -224,10 +267,20 @@
                 pltpu.SemaphoreType.DMA((10, TILES)),
                 pltpu.SemaphoreType.DMA((10, TILES)),
                 pltpu.SemaphoreType.DMA((2, TILES)),
+                pltpu.SemaphoreType.DMA((2, TILES)),
             ],
-            compiler_params=pltpu.CompilerParams(collective_id=0, has_side_effects=True, vmem_limit_bytes=67043328),
+            compiler_params=pltpu.CompilerParams(collective_id=0, has_side_effects=True, vmem_limit_bytes=42 * 2**20),
             cost_estimate=pl.CostEstimate(flops=6 * ROWS * D * FF, bytes_accessed=400 * 2**20, transcendentals=ROWS * FF),
         )(x, w_gate, w_up, w_down)
+        return pl.pallas_call(
+            copy_kernel,
+            out_shape=jax.ShapeDtypeStruct((ROWS, D), bf16),
+            in_specs=[pl.BlockSpec(memory_space=pltpu.VMEM)],
+            out_specs=pl.BlockSpec(memory_space=pl.ANY),
+            scratch_shapes=[pltpu.SemaphoreType.DMA((TILES, PIECES))],
+            compiler_params=pltpu.CompilerParams(vmem_limit_bytes=4 * 2**20),
+            cost_estimate=pl.CostEstimate(flops=0, bytes_accessed=2 * ROWS * D, transcendentals=0),
+        )(whole)
 
     return jax.shard_map(
         step,

time: 273 us -> 263 us (0.963)
  local copies, waits for them, and re-layouts: 18.7 us -> 0 us
  Pallas kernels: 254 us -> 263 us
    unnamed x1 -> x0, local copies, waits for them, and re-layouts: 18.7 us -> none
    pallas_call x1 -> x2, Pallas kernels: 254 us -> 263 us  [the longest x1 255 us: step(): pl.pallas_call(kernel, out_shape=(jax.ShapeDtypeStruct((ROWS, D), bf16),...]
where the time goes in v2:
time: 263 us
  Pallas kernels  263 us (100%)
    pallas_call x1, Pallas kernels, step(): pl.pallas_call(kernel, out_shape=(jax.ShapeDtypeStruct((ROWS, D), bf16),...  255 us
    pallas_call x1, Pallas kernels, step(): pl.pallas_call(copy_kernel, out_shape=jax.ShapeDtypeStruct((ROWS, D), bf1...  7.65 us

profile of v2, /device:TPU:0, one launch (start us, length us, event | category | flops | bytes accessed | tf_op | source)
XLA Modules:
  0.0 262.7 jit_solution(4228131449797112367)
XLA Ops:
  0.0 255.0 %shard_map.46 = (bf16[2048,5376]{1,0:T(8,128)(2,1)}, bf16[14336,768]{1,0:T(8,128)(2,1)S(1)}) custom-call(bf16[2048,5376]{1,0:T(8,128)(2,1)} %x_hbm.1, bf16[5376,2688]{1,0:T(8,128)(2,1)} %wg.1, bf16[5376,2688]{1,0:T(8,128)(2,1)} %wu.1, bf16[2688,5376]{1,0:T(8,128)(2,1)} %wd.1), custom_call_target="tpu_custom_call" | custom-call | flops 177570054144 | bytes 419430400 | tf_op jit(solution)/shard_map/pallas_call | solution.py:249
  255.0 7.6 %shard_map.47 = bf16[2048,5376]{1,0:T(8,128)(2,1)} custom-call(bf16[14336,768]{1,0:T(8,128)(2,1)S(1)} %get-tuple-element.6.whole), custom_call_target="tpu_custom_call" | custom-call | bytes 22020096 | tf_op jit(solution)/shard_map/pallas_call | solution.py:275

commit v3 on v2

--- a/solution.py
+++ b/solution.py
@@ -16,7 +16,7 @@
 T2 = 768
 TILES = FF // T1
 PERIOD = 2 * TILES
-OFFSETS = (2, 4, 6, 8, 10, 12)
+OFFSETS = (2, 5, 7, 9, 12, 14)
 PIECES = 4
 S0, S1, S2, G1, G2, G3 = 0, 1, 3, 5, 7, 9
 
@@ -41,11 +41,6 @@
     pn = me + 1 - 2 * core
     xn = me + 4 - 8 * cx
     yn = me + 2 - 4 * cy
-
-    barrier = pltpu.get_barrier_semaphore()
-    for n in (pn, xn, yn):
-        pl.semaphore_signal(barrier, inc=1, device_id={"tp": n}, device_id_type=MESH)
-    pl.semaphore_wait(barrier, 3)
 
     a = lambda i, j: i * QUARTER + j * SIXTH
     b = lambda j, i: HALF // 2 + j * QUARTER + i * SIXTH
@@ -107,6 +102,10 @@
     f32, bf16 = jnp.float32, jnp.bfloat16
     Q, H = QUARTER, HALF // 2
 
+    def sent(stage, g, j):
+        for c in copies(stage, g, j):
+            c.wait_send()
+
     def stage1(g, j):
         arrive(copies(S0, g, j))
         for i in range(2):
@@ -117,8 +116,7 @@
 
     def stage2(g, j):
         arrive(copies(S1, g, j))
-        for c in copies(S0, g, j):
-            c.wait_send()
+        sent(S0, g, j)
         for i in range(2):
             keep, send = pl.ds(i * H, SIXTH), pl.ds(i * H + SIXTH, SIXTH)
             s2s[j, i] = (acc[j, send] + s1r[j, i, SIXTH:].astype(f32)).astype(bf16)
@@ -127,6 +125,7 @@
 
     def stage3(g, j):
         arrive(copies(S2, g, j))
+        sent(S1, g, j)
         for i in range(2):
             fin[j, i] = (acc[j, pl.ds(i * H, SIXTH)] + s2r[j, i].astype(f32)).astype(bf16)
         start(copies(G1, g, j))
@@ -136,32 +135,44 @@
         for c in own(g, j):
             c.wait()
         arrive(copies(G1, g, j))
+        sent(S2, g, j)
         start(copies(G2, g, j))
 
     def stage5(g, j):
         arrive(copies(G2, g, j))
+        sent(G1, g, j)
         start(copies(G3, g, j))
 
     def stage6(g, j):
         arrive(copies(G3, g, j))
-        for stage in (S1, S2, G1, G2, G3):
-            for c in copies(stage, g, j):
-                c.wait_send()
-
-    def service(tick):
+        sent(G2, g, j)
+        sent(G3, g, j)
+
+    def service(g, j, second):
         for fn, off in zip((stage1, stage2, stage3, stage4, stage5, stage6), OFFSETS):
-            w = tick - TILES - off
-            pos = lax.max(w, 0)
-            g, j = pos // PERIOD, pos % PERIOD
-
-            @pl.when((w >= 0) & (j < TILES) & (g < GROUPS))
-            def _():
-                fn(g, j)
+            groups = GROUPS if fn in (stage1, stage2) else GROUPS - 1
+            for back in range(3):
+                shift = back * PERIOD - off - (0 if second else TILES)
+                if -TILES < shift < TILES and (second or back > 0):
+                    now = (g >= back) & (g - back < groups)
+                    if shift < 0:
+                        now = now & (j + shift >= 0)
+                    if shift > 0:
+                        now = now & (j + shift < TILES)
+
+                    @pl.when(now)
+                    def _():
+                        fn(g - back, j + shift)
 
     start(x_copies(0))
     start(w_copies(0, 0))
     wd_copy(0, 0).start()
 
+    barrier = pltpu.get_barrier_semaphore()
+    for n in (pn, xn, yn):
+        pl.semaphore_signal(barrier, inc=1, device_id={"tp": n}, device_id_type=MESH)
+    pl.semaphore_wait(barrier, 3)
+
     def group(g, _):
         for c in x_copies(g):
             c.wait()
@@ -172,9 +183,9 @@
 
             @pl.when(n + 1 < GROUPS * TILES)
             def _():
-                start(w_copies((j + 1) % TILES, 1 - slot))
-
-            service(g * PERIOD + j)
+                start(w_copies(jnp.where(j + 1 < TILES, j + 1, 0), 1 - slot))
+
+            service(g, j, False)
             for c in w_copies(j, slot):
                 c.wait()
             r = jnp.dot(xbuf[...], whole[wrows(slot), :], preferred_element_type=f32)
@@ -193,9 +204,9 @@
 
             @pl.when(n + 1 < GROUPS * TILES)
             def _():
-                wd_copy((j + 1) % TILES, 1 - slot).start()
-
-            service(g * PERIOD + TILES + j)
+                wd_copy(jnp.where(j + 1 < TILES, j + 1, 0), 1 - slot).start()
+
+            service(g, j, True)
             wd_copy(j, slot).wait()
             r = jnp.dot(hid[...], wdbuf[slot], preferred_element_type=f32)
             acc[j] = r[:HALF]
@@ -212,18 +223,28 @@
         at = pl.ds(pl.multiple_of(j * ROWS + first, GROUP), rows)
         return pltpu.make_async_copy(y.at[pl.ds(first, rows), columns(j)], whole.at[at], vsem.at[sem, j])
 
-    last, full = ROWS - GROUP, 2 * D // ROWS
-    for i in range(OFFSETS[-1]):
-        service(GROUPS * PERIOD + i)
-        if i == 0:
-            for j in range(full):
-                settle(j, 0, last, 0).start()
-        if i == OFFSETS[1]:
-            for j in range(full, TILES):
-                settle(j, 0, last, 0).start()
-        j = i + TILES - OFFSETS[-1]
-        if j >= 0:
-            settle(j, last, GROUP, 1).start()
+    def each(fn, first=0, end=TILES):
+        def step(j, _):
+            fn(j)
+            return 0
+
+        lax.fori_loop(first, end, step, 0)
+
+    last, full, g = ROWS - GROUP, 2 * D // ROWS, GROUPS - 1
+    each(lambda j: stage6(g - 1, j), min(TILES, 3 * TILES - OFFSETS[5]))
+    each(lambda j: settle(j, 0, last, 0).start(), 0, full)
+    each(lambda j: stage1(g, j), TILES - OFFSETS[0])
+    each(lambda j: stage2(g, j), TILES - OFFSETS[1])
+    each(lambda j: settle(j, 0, last, 0).start(), full)
+    each(lambda j: stage3(g, j))
+    each(lambda j: stage4(g, j))
+    each(lambda j: stage5(g, j))
+
+    def finish(j):
+        stage6(g, j)
+        settle(j, last, GROUP, 1).start()
+
+    each(finish)
     for j in range(TILES):
         settle(j, 0, last, 0).wait()
         settle(j, last, GROUP, 1).wait()

time: 263 us -> 257 us (0.977)
  Pallas kernels: 263 us -> 257 us
    pallas_call x1, Pallas kernels: 255 us -> 250 us  [step(): pl.pallas_call(kernel, out_shape=(jax.ShapeDtypeStruct((ROWS, D), bf16),...]
where the time goes in v3:
time: 257 us
  Pallas kernels  257 us (100%)
    pallas_call x1, Pallas kernels, step(): pl.pallas_call(kernel, out_shape=(jax.ShapeDtypeStruct((ROWS, D), bf16),...  250 us
    pallas_call x1, Pallas kernels, step(): pl.pallas_call(copy_kernel, out_shape=jax.ShapeDtypeStruct((ROWS, D), bf1...  7.65 us

profile of v3, /device:TPU:0, one launch (start us, length us, event | category | flops | bytes accessed | tf_op | source)
XLA Modules:
  0.0 257.2 jit_solution(12932813795109136462)
XLA Ops:
  0.0 249.6 %shard_map.46 = (bf16[2048,5376]{1,0:T(8,128)(2,1)}, bf16[14336,768]{1,0:T(8,128)(2,1)S(1)}) custom-call(bf16[2048,5376]{1,0:T(8,128)(2,1)} %x_hbm.1, bf16[5376,2688]{1,0:T(8,128)(2,1)} %wg.1, bf16[5376,2688]{1,0:T(8,128)(2,1)} %wu.1, bf16[2688,5376]{1,0:T(8,128)(2,1)} %wd.1), custom_call_target="tpu_custom_call" | custom-call | flops 177570054144 | bytes 419430400 | tf_op jit(solution)/shard_map/pallas_call | solution.py:270
  249.6 7.6 %shard_map.47 = bf16[2048,5376]{1,0:T(8,128)(2,1)} custom-call(bf16[14336,768]{1,0:T(8,128)(2,1)S(1)} %get-tuple-element.6.whole), custom_call_target="tpu_custom_call" | custom-call | bytes 22020096 | tf_op jit(solution)/shard_map/pallas_call | solution.py:296

commit v4 on v3

--- a/solution.py
+++ b/solution.py
@@ -16,9 +16,9 @@
 T2 = 768
 TILES = FF // T1
 PERIOD = 2 * TILES
-OFFSETS = (2, 5, 7, 9, 12, 14)
+OFFSETS = (2, 4, 7, 9, 12, 14)
 PIECES = 4
-S0, S1, S2, G1, G2, G3 = 0, 1, 3, 5, 7, 9
+S0, S1, S2, G1, G2, G3 = range(6)
 
 
 def gelu(v):
@@ -78,14 +78,14 @@
         if stage == S0:
             return [remote(whole.at[srows(j)], whole.at[rrows(j)], S0, j, pn)]
         if stage == S1:
-            return [remote(s1s.at[j, i], s1r.at[j, i], S1 + i, j, (xn, yn)[i]) for i in range(2)]
+            return [remote(s1s.at[j, i], s1r.at[j, i], S1, j, (xn, yn)[i]) for i in range(2)]
         if stage == S2:
-            return [remote(s2s.at[j, i], s2r.at[j, i], S2 + i, j, (yn, xn)[i]) for i in range(2)]
+            return [remote(s2s.at[j, i], s2r.at[j, i], S2, j, (yn, xn)[i]) for i in range(2)]
         if stage == G1:
-            return [remote(fin.at[j, i], part(g, blocks[4 * i], SIXTH, j), G1 + i, j, (yn, xn)[i]) for i in range(2)]
+            return [remote(fin.at[j, i], part(g, blocks[4 * i], SIXTH, j), G1, j, (yn, xn)[i]) for i in range(2)]
         if stage == G2:
             offs = (cx * QUARTER, HALF // 2 + cy * QUARTER)
-            return [remote(part(g, offs[i], QUARTER, j), part(g, offs[i], QUARTER, j), G2 + i, j, (xn, yn)[i]) for i in range(2)]
+            return [remote(part(g, offs[i], QUARTER, j), part(g, offs[i], QUARTER, j), G2, j, (xn, yn)[i]) for i in range(2)]
         return [remote(part(g, 0, HALF, j), part(g, 0, HALF, j), G3, j, pn)]
 
     def own(g, j):
@@ -95,19 +95,24 @@
         for c in cs:
             c.start()
 
-    def arrive(cs):
-        for c in cs:
-            c.wait_recv()
+    def both(stage, g, j):
+        if stage in (S1, G2):
+            return remote(s1s.at[j], s1r.at[j], stage, j, pn)
+        if stage in (S2, G1):
+            return remote(s2s.at[j], s2r.at[j], stage, j, pn)
+        return copies(stage, g, j)[0]
+
+    def arrive(stage, g, j):
+        both(stage, g, j).wait_recv()
 
     f32, bf16 = jnp.float32, jnp.bfloat16
     Q, H = QUARTER, HALF // 2
 
     def sent(stage, g, j):
-        for c in copies(stage, g, j):
-            c.wait_send()
+        both(stage, g, j).wait_send()
 
     def stage1(g, j):
-        arrive(copies(S0, g, j))
+        arrive(S0, g, j)
         for i in range(2):
             keep, send = pl.ds(i * H, Q), pl.ds(i * H + Q, Q)
             s1s[j, i] = (acc[j, send] + whole[rrows(j, i * H + Q, Q), :].astype(f32)).astype(bf16)
@@ -115,7 +120,7 @@
         start(copies(S1, g, j))
 
     def stage2(g, j):
-        arrive(copies(S1, g, j))
+        arrive(S1, g, j)
         sent(S0, g, j)
         for i in range(2):
             keep, send = pl.ds(i * H, SIXTH), pl.ds(i * H + SIXTH, SIXTH)
@@ -124,7 +129,7 @@
         start(copies(S2, g, j))
 
     def stage3(g, j):
-        arrive(copies(S2, g, j))
+        arrive(S2, g, j)
         sent(S1, g, j)
         for i in range(2):
             fin[j, i] = (acc[j, pl.ds(i * H, SIXTH)] + s2r[j, i].astype(f32)).astype(bf16)
@@ -134,17 +139,17 @@
     def stage4(g, j):
         for c in own(g, j):
             c.wait()
-        arrive(copies(G1, g, j))
+        arrive(G1, g, j)
         sent(S2, g, j)
         start(copies(G2, g, j))
 
     def stage5(g, j):
-        arrive(copies(G2, g, j))
+        arrive(G2, g, j)
         sent(G1, g, j)
         start(copies(G3, g, j))
 
     def stage6(g, j):
-        arrive(copies(G3, g, j))
+        arrive(G3, g, j)
         sent(G2, g, j)
         sent(G3, g, j)
 
@@ -285,8 +290,8 @@
                 pltpu.SemaphoreType.DMA((16,)),
                 pltpu.SemaphoreType.DMA((2, 2)),
                 pltpu.SemaphoreType.DMA((2,)),
-                pltpu.SemaphoreType.DMA((10, TILES)),
-                pltpu.SemaphoreType.DMA((10, TILES)),
+                pltpu.SemaphoreType.DMA((6, TILES)),
+                pltpu.SemaphoreType.DMA((6, TILES)),
                 pltpu.SemaphoreType.DMA((2, TILES)),
                 pltpu.SemaphoreType.DMA((2, TILES)),
             ],

time: 257 us -> 256 us (level)
  no operation moved by 1% of the time
where the time goes in v4:
time: 256 us
  Pallas kernels  256 us (100%)
    pallas_call x1, Pallas kernels, step(): pl.pallas_call(kernel, out_shape=(jax.ShapeDtypeStruct((ROWS, D), bf16),...  248 us
    pallas_call x1, Pallas kernels, step(): pl.pallas_call(copy_kernel, out_shape=jax.ShapeDtypeStruct((ROWS, D), bf1...  7.65 us

profile of v4, /device:TPU:0, one launch (start us, length us, event | category | flops | bytes accessed | tf_op | source)
XLA Modules:
  0.0 256.0 jit_solution(5234508501588382341)
XLA Ops:
  0.0 248.4 %shard_map.46 = (bf16[2048,5376]{1,0:T(8,128)(2,1)}, bf16[14336,768]{1,0:T(8,128)(2,1)S(1)}) custom-call(bf16[2048,5376]{1,0:T(8,128)(2,1)} %x_hbm.1, bf16[5376,2688]{1,0:T(8,128)(2,1)} %wg.1, bf16[5376,2688]{1,0:T(8,128)(2,1)} %wu.1, bf16[2688,5376]{1,0:T(8,128)(2,1)} %wd.1), custom_call_target="tpu_custom_call" | custom-call | flops 177570054144 | bytes 419430400 | tf_op jit(solution)/shard_map/pallas_call | solution.py:275
  248.4 7.6 %shard_map.47 = bf16[2048,5376]{1,0:T(8,128)(2,1)} custom-call(bf16[14336,768]{1,0:T(8,128)(2,1)S(1)} %get-tuple-element.6.whole), custom_call_target="tpu_custom_call" | custom-call | bytes 22020096 | tf_op jit(solution)/shard_map/pallas_call | solution.py:301
